TPU v7x, 32 devices: a whole 2x2x4 slice. The times are simulated.
32 devices in a mesh: mem: 4 (over z), reg: 8 (over y, x, core).
Axes of the slice: x: 2, y: 2, z: 4, core: 2. Of those that a mesh axis runs over, the one named last changes fastest.
Arguments:
- member_values: float32 [40, 32768], P('mem', 'reg'), may hold values from -6 to 6
- obs_value: float32 [32768], P('reg'), may hold values from -6 to 6
- obs_weight: float32 [32768], P('reg'), may hold values from 0.25 to 4
- obs_cell: int32 [32768], P('reg'), may hold values from -1 to 15359, as said below
Outputs:
- deviation: float32 [40, 15360], P('mem', 'reg')
- departure: float32 [15360], P('reg')
- variance: float32 [15360], P('reg')
- error_variance: float32 [15360], P('reg')
- obs_total: int32 [15360], P('reg')
Inputs may be any that keep to these rules, and one draw needn't show every extreme that they name: `obs_cell`: cell c is owned by region c // 1920. The 4096 slots of one region are 8 blocks of 512 slots, block r holding only cells owned by region r, live slots first and -1 in the empty ones. Every block has at least 128 live slots; one owner's block is full in every region.
All inputs are finite; a program needn't handle non-finite values.
Results may differ from a plain program's by a relative error of at most 0.0003.
Values sent between devices are 32-bit elements; how exact they have to be, the bound alone decides.
No kernel may reach another device: no remote copies, remote signals or barrier semaphores. Data moves between devices by JAX's collectives and lax.ppermute only.
A program may use at most 64 MiB of HBM per device.

v0:
```python
import jax
import jax.numpy as jnp
from jax import lax
from jax.sharding import PartitionSpec as P

CELL_DEV = 1920


def shards(member_values, obs_value, obs_weight, obs_cell):
    regions = lax.axis_size("reg")
    groups = lax.axis_size("mem")
    obs_dev = obs_cell.shape[0]
    capacity = obs_dev // regions
    live = obs_cell >= 0
    weight = jnp.where(live, obs_weight, jnp.float32(0.0))
    local_cell = jnp.where(live, obs_cell % CELL_DEV, 0).astype(jnp.float32)
    weighted_members = member_values * weight[None, :]
    meta_rows = jnp.stack([weight * obs_value, weight, local_cell])
    member_buffer = weighted_members.reshape(weighted_members.shape[0], regions, capacity)
    meta_buffer = meta_rows.reshape(3, regions, capacity)
    payload = jnp.concatenate([member_buffer, meta_buffer], 0)
    received = lax.all_to_all(payload, "reg", split_axis=1, concat_axis=1, tiled=True)
    received = received.reshape(received.shape[0], -1)
    members_in = received[:-3]
    meta_in = received[-3:]
    cell_in = meta_in[2].astype(jnp.int32)
    filled_flag = (meta_in[1] > 0).astype(jnp.float32)
    columns = jnp.concatenate([members_in, meta_in[:2], filled_flag[None, :]], 0)
    total_rows = columns.shape[1]
    block_rows = 1024
    column_blocks = columns.reshape(
        columns.shape[0], total_rows // block_rows, block_rows
    ).transpose(1, 0, 2)
    cell_blocks = cell_in.reshape(total_rows // block_rows, block_rows)
    cell_range = jnp.arange(CELL_DEV, dtype=jnp.int32)

    def add_block(carry, inputs):
        block_columns, block_cells = inputs
        one_hot = (block_cells[:, None] == cell_range[None, :]).astype(jnp.float32)
        return (
            carry
            + jnp.dot(
                block_columns,
                one_hot,
                precision=lax.Precision.HIGHEST,
                preferred_element_type=jnp.float32,
            ),
            None,
        )

    start_sums = jnp.zeros((columns.shape[0], CELL_DEV), jnp.float32)
    cell_sums, _ = lax.scan(add_block, start_sums, (column_blocks, cell_blocks))
    counted = cell_sums[-1]
    filled = counted > 0
    weight_total = jnp.where(filled, cell_sums[-2], jnp.float32(1.0))
    superob = cell_sums[:-3] / weight_total[None, :]
    observed_mean = cell_sums[-3] / weight_total
    ensemble = member_values.shape[0] * groups
    moment_one, moment_two = lax.psum((jnp.sum(superob, 0), jnp.sum(superob * superob, 0)), "mem")
    ens_mean = moment_one / ensemble
    deviation = superob - ens_mean[None, :]
    variance = (moment_two - moment_one * ens_mean) / (ensemble - 1)
    departure = observed_mean - ens_mean
    error_variance = jnp.where(filled, 1.0 / weight_total, jnp.float32(0.0))
    return (deviation, departure, variance, error_variance, counted.astype(jnp.int32))


def solution(mesh):
    return jax.shard_map(
        shards,
        mesh=mesh,
        in_specs=(P("mem", "reg"), P("reg"), P("reg"), P("reg")),
        out_specs=(P("mem", "reg"), P("reg"), P("reg"), P("reg"), P("reg")),
        check_vma=False,
    )
```

profile of v0, /device:TPU:0, one launch (start us, length us, event | category | flops | bytes accessed | tf_op | source)
XLA Modules:
  0.0 48.5 jit_solution(72465091545235863)
XLA Ops:
  0.6 0.7 %fusion.6 = f32[4096]{0:T(1024)S(1)} fusion(s32[4096]{0:T(1024)} %param.9), kind=kLoop, calls=%fused_computation.17 | loop fusion | flops 36864 | bytes 32768 | tf_op jit(solution)/shard_map/convert_element_type | solution.py:16
  1.4 0.8 %fusion.11 = (f32[4096]{0:T(1024)S(1)}, f32[4096]{0:T(1024)S(1)}) fusion(f32[4096]{0:T(1024)} %param.7, f32[4096]{0:T(1024)} %param.8, s32[4096]{0:T(1024)} %param.9), kind=kLoop, calls=%fused_computation.34 | loop fusion | flops 12288 | bytes 81920 | tf_op jit(solution)/shard_map/mul | solution.py:18
  2.1 1.0 %broadcast_multiply_fusion = f32[10,4096]{1,0:T(8,128)S(1)} fusion(f32[10,4096]{1,0:T(8,128)} %param.6, f32[4096]{0:T(1024)S(1)} %get-tuple-element.78), kind=kLoop, calls=%fused_computation.10 | loop fusion | flops 40960 | bytes 344064 | tf_op jit(solution)/shard_map/mul | solution.py:17
  3.1 0.2 copy.18
  3.3 0.8 %copy.13 = f32[13,8,512]{2,0,1:T(8,128)} copy(f32[13,8,512]{2,1,0:T(8,128)S(1)} %pad_maximum_fusion) | data formatting | bytes 425984 | tf_op jit(solution)/shard_map/concatenate | solution.py:21
  4.2 5.2 %all-to-all-start = ((f32[13,8,512]{2,0,1:T(8,128)}), f32[13,8,512]{2,0,1:T(8,128)S(1)}, u32[]{:S(2)}, u32[]{:S(2)}) async-start(f32[13,8,512]{2,0,1:T(8,128)} %copy.13), calls=%async_computation | async-start | bytes 524288 | tf_op jit(solution)/shard_map/all_to_all | solution.py:22
  9.4 6.9 %all-to-all-done = f32[13,8,512]{2,0,1:T(8,128)S(1)} async-done(((f32[13,8,512]{2,0,1:T(8,128)}), f32[13,8,512]{2,0,1:T(8,128)S(1)}, u32[]{:S(2)}, u32[]{:S(2)}) %all-to-all-start) | async-done | bytes 213024 | tf_op jit(solution)/shard_map/all_to_all | solution.py:22
  16.3 0.1 copy.14
  16.4 0.1 concatenate.14
  16.5 0.1 fusion.7
  16.6 0.1 fusion.8
  16.7 0.1 maximum_bitcast_fusion
  16.8 10.7 %while.11 = (s32[]{:T(128)}, f32[13,1920]{1,0:T(8,128)S(1)}, f32[4,13,1024]{2,0,1:T(4,128)S(1)}, s32[4,1024]{1,0:T(4,128)S(1)}, s32[]{:T(128)}, /*index=5*/s32[]{:T(128)}) while((s32[]{:T(128)}, f32[13,1920]{1,0:T(8,128)S(1)}, f32[4,13,1024]{2,0,1:T(4,128)S(1)}, s32[4,1024]{1,0:T(4,128)S(1)}, s32[]{:T(128)}, ...), condition=%wide.region_1.2_spmd.clone, body=%wide.region_0.1_spmd.clone.sunk | while | flops 308724480 | bytes 371799 | solution.py:52
  16.8 0.1 constant_dynamic-slice_fusion.5
  16.9 2.6 %fusion.13 = f32[13,1920]{1,0:T(8,128)S(1)} fusion(s32[1024]{0:T(1024)S(1)} %bitcast.17, f32[13,1920]{1,0:T(8,128)S(1)} %get-tuple-element.115, f32[1,13,1024]{2,0,1:T(1,128)S(1)} %constant_dynamic-slice_fusion.5, pred[]{:T(512)S(6)} %compare.3), kind=kOutput, calls=%fused_computation.4.clone.1 | convolution fusion | flops 308724480 | bytes 257025 | tf_op jit(solution)/shard_map/while/body/eval_jaxpr/dot_general | solution.py:42
  19.4 0.1 constant_dynamic-slice_fusion.5
  19.5 2.6 %fusion.13 = f32[13,1920]{1,0:T(8,128)S(1)} fusion(s32[1024]{0:T(1024)S(1)} %bitcast.17, f32[13,1920]{1,0:T(8,128)S(1)} %get-tuple-element.115, f32[1,13,1024]{2,0,1:T(1,128)S(1)} %constant_dynamic-slice_fusion.5, pred[]{:T(512)S(6)} %compare.3), kind=kOutput, calls=%fused_computation.4.clone.1 | convolution fusion | flops 308724480 | bytes 257025 | tf_op jit(solution)/shard_map/while/body/eval_jaxpr/dot_general | solution.py:42
  22.1 0.1 constant_dynamic-slice_fusion.5
  22.2 2.6 %fusion.13 = f32[13,1920]{1,0:T(8,128)S(1)} fusion(s32[1024]{0:T(1024)S(1)} %bitcast.17, f32[13,1920]{1,0:T(8,128)S(1)} %get-tuple-element.115, f32[1,13,1024]{2,0,1:T(1,128)S(1)} %constant_dynamic-slice_fusion.5, pred[]{:T(512)S(6)} %compare.3), kind=kOutput, calls=%fused_computation.4.clone.1 | convolution fusion | flops 308724480 | bytes 257025 | tf_op jit(solution)/shard_map/while/body/eval_jaxpr/dot_general | solution.py:42
  24.8 0.1 constant_dynamic-slice_fusion.5
  24.9 2.6 %fusion.13 = f32[13,1920]{1,0:T(8,128)S(1)} fusion(s32[1024]{0:T(1024)S(1)} %bitcast.17, f32[13,1920]{1,0:T(8,128)S(1)} %get-tuple-element.115, f32[1,13,1024]{2,0,1:T(1,128)S(1)} %constant_dynamic-slice_fusion.5, pred[]{:T(512)S(6)} %compare.3), kind=kOutput, calls=%fused_computation.4.clone.1 | convolution fusion | flops 308724480 | bytes 257025 | tf_op jit(solution)/shard_map/while/body/eval_jaxpr/dot_general | solution.py:42
  27.5 0.1 slice_reduce_fusion.1
  27.6 0.6 %convert_reduce_fusion = s32[1920]{0:T(1024)} fusion(f32[13,1920]{1,0:T(8,128)S(1)} %get-tuple-element.32), kind=kLoop, calls=%fused_computation.29 | loop fusion | flops 1920 | bytes 15360 | tf_op jit(solution)/shard_map/convert_element_type | solution.py:65
  28.2 0.1 multiply_reduce_fusion
  28.3 19.0 %all-reduce = (f32[1920]{0:T(1024)S(1)}, f32[1920]{0:T(1024)S(1)}) all-reduce(f32[1920]{0:T(1024)S(1)} %get-tuple-element.63, f32[1920]{0:T(1024)S(1)} %get-tuple-element.62), channel_id=1, replica_groups=mesh['mem'=4,'reg'=8] {'mem'}, use_global_device_ids=true, to_apply=%region_3.4 | all-reduce | flops 3840 | bytes 30720 | tf_op jit(solution)/shard_map/psum | solution.py:59
  47.3 0.6 %divide_select_fusion = (f32[1920]{0:T(1024)}, f32[1920]{0:T(1024)}, f32[1920]{0:T(1024)}, f32[1920]{0:T(1024)S(1)}) fusion(pred[1920]{0:T(1024)(128)(4,1)S(1)} %compare_reduce_fusion, f32[1920]{0:T(1024)S(1)} %get-tuple-element.64, f32[1920]{0:T(1024)S(1)} %get-tuple-element.75, f32[1920]{0:T(1024)S(1)} %get-tuple-element.65, f32[1920]{0:T(1024)S(1)} %get-tuple-element.76), kind=kLoop, calls=%fused_computation.23 | loop fusion | flops 17280 | bytes 63360 | tf_op jit(solution)/shard_map/jit(_where)/select_n | solution.py:64
  47.9 0.7 %broadcast_subtract_fusion = f32[10,1920]{1,0:T(8,128)} fusion(f32[1920]{0:T(1024)S(1)} %get-tuple-element.82, f32[1920]{0:T(1024)S(1)} %get-tuple-element.66, f32[13,1920]{1,0:T(8,128)S(1)} %get-tuple-element.32), kind=kLoop, calls=%fused_computation.14 | loop fusion | flops 38400 | bytes 168960 | tf_op jit(solution)/shard_map/sub | solution.py:61
  (16 shorter events, 0.2 us)
Async XLA Ops:
  4.2 12.1 %all-to-all-start = ((f32[13,8,512]{2,0,1:T(8,128)}), f32[13,8,512]{2,0,1:T(8,128)S(1)}, u32[]{:S(2)}, u32[]{:S(2)}) async-start(f32[13,8,512]{2,0,1:T(8,128)} %copy.13), calls=%async_computation | async-start | bytes 524288 | tf_op jit(solution)/shard_map/all_to_all | solution.py:22
where the time goes:
time: 49 us; the launch traced here: 48.5 us
  blocking collectives  19 us (39%)
  matrix products  10.3 us (21%)
  waiting for transfers between devices  6.9 us (14%)
  starting transfers between devices  5.2 us (11%)
  other arithmetic  4.73 us (10%)
  local copies, waits for them, and re-layouts  1.52 us (3%)
  between operations  0.77 us (2%)
    psum x1, blocking collectives, shards(): lax.psum((jnp.sum(superob, 0), jnp.sum(superob * superob, 0)), 'mem')  19 us
    dot_general x4, matrix products, add_block(): jnp.dot(block_columns, one_hot, precision=lax.Precision.HIGHEST, preferre...  10.3 us
    all_to_all x1, waiting for transfers between devices, shards(): lax.all_to_all(payload, 'reg', split_axis=1, concat_axis=1, tiled=True)  6.9 us
    all_to_all x1, starting transfers between devices, shards(): lax.all_to_all(payload, 'reg', split_axis=1, concat_axis=1, tiled=True)  5.2 us
  transfers between devices with their start and end apart: 1, of which 1 were waited for; matrix products, arithmetic and copies ran while one was open for 0% of the time, Pallas kernels for 0%

commit v1 on v0

--- a/solution.py
+++ b/solution.py
@@ -19,7 +19,15 @@
     member_buffer = weighted_members.reshape(weighted_members.shape[0], regions, capacity)
     meta_buffer = meta_rows.reshape(3, regions, capacity)
     payload = jnp.concatenate([member_buffer, meta_buffer], 0)
-    received = lax.all_to_all(payload, "reg", split_axis=1, concat_axis=1, tiled=True)
+    received = jnp.concatenate(
+        jax.lax.all_to_all(
+            jnp.stack(jnp.split(payload, jax.lax.axis_size("reg"), 1), 0),
+            axis_name="reg",
+            split_axis=0,
+            concat_axis=0,
+        ),
+        1,
+    )
     received = received.reshape(received.shape[0], -1)
     members_in = received[:-3]
     meta_in = received[-3:]

time: 49 us -> 52.6 us (1.073)
  local copies, waits for them, and re-layouts: 1.52 us -> 5.67 us
    unnamed x1 -> x11, local copies, waits for them, and re-layouts: 0.16 us -> 4.57 us
    concatenate x1, local copies, waits for them, and re-layouts: 0.82 us -> 0.01 us  [shards(): payload = jnp.concatenate([member_buffer, meta_buffer], 0)]
    another operation x0 -> x1, local copies, waits for them, and re-layouts: none -> 0.64 us  [shards(): jnp.stack(jnp.split(payload, jax.lax.axis_size('reg'), 1), 0)]
    all_to_all x1, waiting for transfers between devices: 6.9 us -> 6.38 us  [shards(): jax.lax.all_to_all(jnp.stack(jnp.split(payload, jax.lax.axis_size('reg'),...]
where the time goes in v1:
time: 52.6 us; the launch traced here: 52.2 us
  blocking collectives  19 us (36%)
  matrix products  10.3 us (20%)
  waiting for transfers between devices  6.38 us (12%)
  local copies, waits for them, and re-layouts  5.67 us (11%)
  starting transfers between devices  5.2 us (10%)
  other arithmetic  4.69 us (9%)
  between operations  0.8 us (2%)
    psum x1, blocking collectives, shards(): lax.psum((jnp.sum(superob, 0), jnp.sum(superob * superob, 0)), 'mem')  19 us
    dot_general x4, matrix products, add_block(): jnp.dot(block_columns, one_hot, precision=lax.Precision.HIGHEST, preferre...  10.3 us
    all_to_all x1, waiting for transfers between devices, shards(): jax.lax.all_to_all(jnp.stack(jnp.split(payload, jax.lax.axis_size('reg'),...  6.38 us
    all_to_all x1, starting transfers between devices, shards(): jax.lax.all_to_all(jnp.stack(jnp.split(payload, jax.lax.axis_size('reg'),...  5.2 us
    unnamed x11, local copies, waits for them, and re-layouts  4.57 us
  transfers between devices with their start and end apart: 1, of which 1 were waited for; matrix products, arithmetic and copies ran while one was open for 0% of the time, Pallas kernels for 0%

profile of v1, /device:TPU:0, one launch (start us, length us, event | category | flops | bytes accessed | tf_op | source)
XLA Modules:
  0.0 52.2 jit_solution(6257856865962109668)
XLA Ops:
  0.6 0.7 %fusion.14 = f32[4096]{0:T(1024)S(1)} fusion(s32[4096]{0:T(1024)} %param.9), kind=kLoop, calls=%fused_computation.36 | loop fusion | flops 36864 | bytes 32768 | tf_op jit(solution)/shard_map/convert_element_type | solution.py:16
  1.4 0.8 %fusion.19 = (f32[4096]{0:T(1024)S(1)}, f32[4096]{0:T(1024)S(1)}) fusion(f32[4096]{0:T(1024)} %param.7, f32[4096]{0:T(1024)} %param.8, s32[4096]{0:T(1024)} %param.9), kind=kLoop, calls=%fused_computation.53 | loop fusion | flops 12288 | bytes 81920 | tf_op jit(solution)/shard_map/mul | solution.py:18
  2.1 1.0 %broadcast_multiply_fusion = f32[10,4096]{1,0:T(8,128)S(1)} fusion(f32[10,4096]{1,0:T(8,128)} %param.6, f32[4096]{0:T(1024)S(1)} %get-tuple-element.82), kind=kLoop, calls=%fused_computation.10 | loop fusion | flops 40960 | bytes 344064 | tf_op jit(solution)/shard_map/mul | solution.py:17
  3.1 0.2 copy.35
  3.4 0.6 %fusion.12 = f32[8,13,1,512]{3,2,1,0:T(1,128)} fusion(f32[13,8,512]{2,1,0:T(8,128)S(1)} %constant_dynamic-update-slice_fusion), kind=kLoop, calls=%fused_computation.30 | loop fusion | bytes 53248
  4.0 0.6 %fusion.11 = f32[8,13,1,512]{3,2,1,0:T(1,128)} fusion(f32[8,13,1,512]{3,2,1,0:T(1,128)} %fusion.12, f32[13,8,512]{2,1,0:T(8,128)S(1)} %constant_dynamic-update-slice_fusion), kind=kLoop, calls=%fused_computation.28 | loop fusion | bytes 53248
  4.6 0.6 %fusion.10 = f32[8,13,1,512]{3,2,1,0:T(1,128)} fusion(f32[8,13,1,512]{3,2,1,0:T(1,128)} %fusion.11, f32[13,8,512]{2,1,0:T(8,128)S(1)} %constant_dynamic-update-slice_fusion), kind=kLoop, calls=%fused_computation.26 | loop fusion | bytes 53248
  5.2 0.6 %fusion.9 = f32[8,13,1,512]{3,2,1,0:T(1,128)} fusion(f32[8,13,1,512]{3,2,1,0:T(1,128)} %fusion.10, f32[13,8,512]{2,1,0:T(8,128)S(1)} %constant_dynamic-update-slice_fusion), kind=kLoop, calls=%fused_computation.24 | loop fusion | bytes 53248
  5.9 0.6 %fusion.8 = f32[8,13,1,512]{3,2,1,0:T(1,128)} fusion(f32[8,13,1,512]{3,2,1,0:T(1,128)} %fusion.9, f32[13,8,512]{2,1,0:T(8,128)S(1)} %constant_dynamic-update-slice_fusion), kind=kLoop, calls=%fused_computation.22 | loop fusion | bytes 53248
  6.5 0.6 %fusion.7 = f32[8,13,1,512]{3,2,1,0:T(1,128)} fusion(f32[8,13,1,512]{3,2,1,0:T(1,128)} %fusion.8, f32[13,8,512]{2,1,0:T(8,128)S(1)} %constant_dynamic-update-slice_fusion), kind=kLoop, calls=%fused_computation.20 | loop fusion | bytes 53248
  7.1 0.6 %fusion.6 = f32[8,13,1,512]{3,2,1,0:T(1,128)} fusion(f32[8,13,1,512]{3,2,1,0:T(1,128)} %fusion.7, f32[13,8,512]{2,1,0:T(8,128)S(1)} %constant_dynamic-update-slice_fusion), kind=kLoop, calls=%fused_computation.18 | loop fusion | bytes 53248
  7.7 0.6 %fusion.5 = f32[8,13,1,512]{3,2,1,0:T(1,128)} fusion(f32[8,13,1,512]{3,2,1,0:T(1,128)} %fusion.6, f32[13,8,512]{2,1,0:T(8,128)S(1)} %constant_dynamic-update-slice_fusion), kind=kLoop, calls=%fused_computation.16 | loop fusion | bytes 53248 | tf_op jit(solution)/shard_map/stack | solution.py:24
  8.4 5.2 %all-to-all-start = ((f32[8,13,1,512]{3,2,1,0:T(1,128)}), f32[8,13,1,512]{3,2,1,0:T(1,128)S(1)}, u32[]{:S(2)}, u32[]{:S(2)}) async-start(f32[8,13,1,512]{3,2,1,0:T(1,128)} %fusion.5), calls=%async_computation | async-start | bytes 425984 | tf_op jit(solution)/shard_map/all_to_all | solution.py:23
  13.6 6.4 %all-to-all-done = f32[8,13,1,512]{3,2,1,0:T(1,128)S(1)} async-done(((f32[8,13,1,512]{3,2,1,0:T(1,128)}), f32[8,13,1,512]{3,2,1,0:T(1,128)S(1)}, u32[]{:S(2)}, u32[]{:S(2)}) %all-to-all-start) | async-done | bytes 213024 | tf_op jit(solution)/shard_map/all_to_all | solution.py:23
  20.1 0.1 concatenate.14
  20.3 0.1 maximum_bitcast_fusion
  20.4 10.7 %while.11 = (s32[]{:T(128)}, f32[13,1920]{1,0:T(8,128)S(1)}, f32[4,13,1024]{2,0,1:T(4,128)S(1)}, s32[4,1024]{1,0:T(4,128)S(1)}, s32[]{:T(128)}, /*index=5*/s32[]{:T(128)}) while((s32[]{:T(128)}, f32[13,1920]{1,0:T(8,128)S(1)}, f32[4,13,1024]{2,0,1:T(4,128)S(1)}, s32[4,1024]{1,0:T(4,128)S(1)}, s32[]{:T(128)}, ...), condition=%wide.region_1.2_spmd.clone, body=%wide.region_0.1_spmd.clone.sunk | while | flops 308724480 | bytes 371799 | solution.py:60
  20.4 0.1 constant_dynamic-slice_fusion.5
  20.5 2.6 %fusion.21 = f32[13,1920]{1,0:T(8,128)S(1)} fusion(s32[1024]{0:T(1024)S(1)} %bitcast.60, f32[13,1920]{1,0:T(8,128)S(1)} %get-tuple-element.119, f32[1,13,1024]{2,0,1:T(1,128)S(1)} %constant_dynamic-slice_fusion.5, pred[]{:T(512)S(6)} %compare.3), kind=kOutput, calls=%fused_computation.4.clone.1 | convolution fusion | flops 308724480 | bytes 257025 | tf_op jit(solution)/shard_map/while/body/eval_jaxpr/dot_general | solution.py:50
  23.1 0.1 constant_dynamic-slice_fusion.5
  23.1 2.6 %fusion.21 = f32[13,1920]{1,0:T(8,128)S(1)} fusion(s32[1024]{0:T(1024)S(1)} %bitcast.60, f32[13,1920]{1,0:T(8,128)S(1)} %get-tuple-element.119, f32[1,13,1024]{2,0,1:T(1,128)S(1)} %constant_dynamic-slice_fusion.5, pred[]{:T(512)S(6)} %compare.3), kind=kOutput, calls=%fused_computation.4.clone.1 | convolution fusion | flops 308724480 | bytes 257025 | tf_op jit(solution)/shard_map/while/body/eval_jaxpr/dot_general | solution.py:50
  25.7 0.1 constant_dynamic-slice_fusion.5
  25.8 2.6 %fusion.21 = f32[13,1920]{1,0:T(8,128)S(1)} fusion(s32[1024]{0:T(1024)S(1)} %bitcast.60, f32[13,1920]{1,0:T(8,128)S(1)} %get-tuple-element.119, f32[1,13,1024]{2,0,1:T(1,128)S(1)} %constant_dynamic-slice_fusion.5, pred[]{:T(512)S(6)} %compare.3), kind=kOutput, calls=%fused_computation.4.clone.1 | convolution fusion | flops 308724480 | bytes 257025 | tf_op jit(solution)/shard_map/while/body/eval_jaxpr/dot_general | solution.py:50
  28.4 0.1 constant_dynamic-slice_fusion.5
  28.5 2.6 %fusion.21 = f32[13,1920]{1,0:T(8,128)S(1)} fusion(s32[1024]{0:T(1024)S(1)} %bitcast.60, f32[13,1920]{1,0:T(8,128)S(1)} %get-tuple-element.119, f32[1,13,1024]{2,0,1:T(1,128)S(1)} %constant_dynamic-slice_fusion.5, pred[]{:T(512)S(6)} %compare.3), kind=kOutput, calls=%fused_computation.4.clone.1 | convolution fusion | flops 308724480 | bytes 257025 | tf_op jit(solution)/shard_map/while/body/eval_jaxpr/dot_general | solution.py:50
  31.1 0.1 slice_reduce_fusion.1
  31.2 0.6 %convert_reduce_fusion = s32[1920]{0:T(1024)} fusion(f32[13,1920]{1,0:T(8,128)S(1)} %get-tuple-element.32), kind=kLoop, calls=%fused_computation.48 | loop fusion | flops 1920 | bytes 15360 | tf_op jit(solution)/shard_map/convert_element_type | solution.py:73
  31.8 0.1 multiply_reduce_fusion
  31.9 19.0 %all-reduce = (f32[1920]{0:T(1024)S(1)}, f32[1920]{0:T(1024)S(1)}) all-reduce(f32[1920]{0:T(1024)S(1)} %get-tuple-element.67, f32[1920]{0:T(1024)S(1)} %get-tuple-element.66), channel_id=1, replica_groups=mesh['mem'=4,'reg'=8] {'mem'}, use_global_device_ids=true, to_apply=%region_3.4 | all-reduce | flops 3840 | bytes 30720 | tf_op jit(solution)/shard_map/psum | solution.py:67
  50.9 0.6 %divide_select_fusion = (f32[1920]{0:T(1024)}, f32[1920]{0:T(1024)}, f32[1920]{0:T(1024)}, f32[1920]{0:T(1024)S(1)}) fusion(pred[1920]{0:T(1024)(128)(4,1)S(1)} %compare_reduce_fusion, f32[1920]{0:T(1024)S(1)} %get-tuple-element.68, f32[1920]{0:T(1024)S(1)} %get-tuple-element.79, f32[1920]{0:T(1024)S(1)} %get-tuple-element.69, f32[1920]{0:T(1024)S(1)} %get-tuple-element.80), kind=kLoop, calls=%fused_computation.42 | loop fusion | flops 17280 | bytes 63360 | tf_op jit(solution)/shard_map/jit(_where)/select_n | solution.py:72
  51.5 0.7 %broadcast_subtract_fusion = f32[10,1920]{1,0:T(8,128)} fusion(f32[1920]{0:T(1024)S(1)} %get-tuple-element.86, f32[1920]{0:T(1024)S(1)} %get-tuple-element.70, f32[13,1920]{1,0:T(8,128)S(1)} %get-tuple-element.32), kind=kLoop, calls=%fused_computation.14 | loop fusion | flops 38400 | bytes 168960 | tf_op jit(solution)/shard_map/sub | solution.py:69
  (22 shorter events, 0.3 us)
Async XLA Ops:
  8.4 11.6 %all-to-all-start = ((f32[8,13,1,512]{3,2,1,0:T(1,128)}), f32[8,13,1,512]{3,2,1,0:T(1,128)S(1)}, u32[]{:S(2)}, u32[]{:S(2)}) async-start(f32[8,13,1,512]{3,2,1,0:T(1,128)} %fusion.5), calls=%async_computation | async-start | bytes 425984 | tf_op jit(solution)/shard_map/all_to_all | solution.py:23
